TPU v7x, 32 devices: a whole 2x2x4 slice. The times are simulated.
32 devices in a mesh: gx: 8 (over z, core), gz: 4 (over y, x).
Axes of the slice: x: 2, y: 2, z: 4, core: 2. Of those that a mesh axis runs over, the one named last changes fastest.
Arguments:
- view_index: int32 [1], replicated, may hold values from 0 to 5
- psf_taps: float32 [6, 3, 31], replicated, may hold values from 0.1 to 1
- extents: int32 [6, 3], replicated, may hold values from 4 to 15
- estimate: float32 [16, 256, 1024], P(None, 'gz', 'gx'), may hold values from 0.5 to 2
- measured: float32 [16, 256, 1024], P(None, 'gz', 'gx'), may hold values from 0.25 to 4
Outputs:
- upsampled: float32 [16, 1024, 1024], P('gz', None, 'gx')
All inputs are finite; a program needn't handle non-finite values.
Results may differ from a plain program's by a relative error of at most 0.004.
Values may be sent and summed in bfloat16 or wider, within the bound.
A program may use at most 64 MiB of HBM per device.

v0:
```python
import math

import jax
import jax.numpy as jnp
from jax import lax
from jax.sharding import PartitionSpec as P

HALF = 15
TAPS = 31
UP = 4


def extended(cells, sides, width):
    for axis, dim in sides:
        count = lax.axis_size(axis)
        ends = count - 1
        head = lax.slice_in_dim(cells, 0, width, axis=dim)
        tail = lax.slice_in_dim(cells, cells.shape[dim] - width, cells.shape[dim], axis=dim)
        cells = jnp.concatenate(
            [
                lax.ppermute(tail, axis, [(i, (i + 1) % count) for i in range(ends)]),
                cells,
                lax.ppermute(head, axis, [((i + 1) % count, i) for i in range(ends)]),
            ],
            axis=dim,
        )
    return cells


def pick_kernels(view_index, psf_taps, extents):
    selector = (jnp.arange(psf_taps.shape[0], dtype=jnp.int32) == view_index[0]).astype(jnp.float32)
    picked = jnp.sum(psf_taps * selector[:, None, None], axis=0)
    reach = jnp.sum(extents.astype(jnp.float32) * selector[:, None], axis=0)
    offsets = (jnp.arange(TAPS, dtype=jnp.int32) - HALF).astype(jnp.float32)
    kernels = []
    for axis_id in range(3):
        unnormalized_taps = picked[axis_id] * (jnp.abs(offsets) <= reach[axis_id]).astype(
            jnp.float32
        )
        kernels.append(unnormalized_taps / jnp.sum(unnormalized_taps))
    return kernels


def smear_valid(padded, kernel, axis_dim):
    length = padded.shape[axis_dim] - 2 * HALF
    total = jnp.zeros(
        padded.shape[:axis_dim] + (length,) + padded.shape[axis_dim + 1 :], jnp.float32
    )
    for tap_index in range(TAPS):
        total = total + kernel[tap_index] * lax.slice_in_dim(
            padded, tap_index, tap_index + length, axis=axis_dim
        )
    return total


def local_convolve(volume, kernel, axis_dim):
    pad_widths = [(0, 0), (0, 0), (0, 0)]
    pad_widths[axis_dim] = (HALF, HALF)
    return smear_valid(jnp.pad(volume, pad_widths), kernel, axis_dim)


def blur(volume, kernels):
    wide = extended(volume, (("gx", 2),), HALF)
    section_one = smear_valid(wide, kernels[0], 2)
    section_two = local_convolve(section_one, kernels[1], 0)
    tall = extended(section_two, (("gz", 1),), HALF)
    return smear_valid(tall, kernels[2], 1)


def build_table(first_row, count_of_rows, length):
    row_ids = first_row + jnp.arange(count_of_rows, dtype=jnp.int32)[:, None]
    column_numbers = jnp.arange(length, dtype=jnp.int32)[None, :]
    offset_units = jnp.mod(row_ids - UP * column_numbers, UP * length)
    sine_part = jnp.sin(jnp.pi * jnp.mod(offset_units, 2 * UP).astype(jnp.float32) / UP)
    tangent_part = length * jnp.tan(jnp.pi * offset_units.astype(jnp.float32) / (UP * length))
    on_grid = jnp.mod(offset_units, UP) == 0
    guarded_denominator = jnp.where(on_grid, jnp.float32(1.0), tangent_part)
    entries = jnp.where(
        on_grid,
        jnp.where(offset_units == 0, jnp.float32(1.0), jnp.float32(0.0)),
        sine_part / guarded_denominator,
    )
    return entries.astype(jnp.bfloat16)


def upsample(depth_columns):
    length = depth_columns.shape[1]
    rows_out = length * UP
    block_rows = math.gcd(rows_out, 512)
    block_count = rows_out // block_rows

    def block_out(block_index):
        slab_lookup_table = build_table(block_index * block_rows, block_rows, length)
        return jnp.einsum(
            "ep,hps->hes", slab_lookup_table, depth_columns, preferred_element_type=jnp.float32
        )

    pieces = lax.map(block_out, jnp.arange(block_count, dtype=jnp.int32))
    return jnp.transpose(pieces, (1, 0, 2, 3)).reshape(
        depth_columns.shape[0], rows_out, depth_columns.shape[2]
    )


def on_device(view_index, psf_taps, extents, estimate, measured):
    kernels = pick_kernels(view_index, psf_taps, extents)
    adjoint_direction = [kernel[::-1] for kernel in kernels]
    blurred = blur(estimate, kernels)
    quotient = measured / blurred
    correction = blur(quotient, adjoint_direction)
    rounded = (estimate * correction).astype(jnp.bfloat16)
    return upsample(lax.all_to_all(rounded, "gz", split_axis=0, concat_axis=1, tiled=True))


def solution(mesh):
    return jax.shard_map(
        on_device,
        mesh=mesh,
        in_specs=(P(), P(), P(), P(None, "gz", "gx"), P(None, "gz", "gx")),
        out_specs=P("gz", None, "gx"),
        check_vma=False,
    )
```

profile of v0, /device:TPU:8, one launch (start us, length us, event | category | flops | bytes accessed | tf_op | source)
XLA Modules:
  0.0 214.4 jit_solution(3570523419888991835)
XLA Ops:
  0.0 2.2 %fusion.490 = (f32[16,64,15]{2,1,0:T(8,128)}, f32[16,64,15]{2,1,0:T(8,128)S(1)}) fusion(f32[16,64,128]{2,1,0:T(8,128)} %param.10), kind=kLoop, calls=%fused_computation.795 | loop fusion | bytes 245760 | tf_op jit(solution)/shard_map/slice | solution.py:17
  2.2 1.9 collective-permute-start.1
  4.1 2.4 %collective-permute-start = (f32[16,64,15]{2,1,0:T(8,128)S(1)}, f32[16,64,15]{2,1,0:T(8,128)S(1)}, u32[]{:S(2)}, u32[]{:S(2)}) collective-permute-start(f32[16,64,15]{2,1,0:T(8,128)S(1)} %get-tuple-element.110), channel_id=1, source_target_pairs={{0,4},{4,8},{8,12},{12,16},{16,20},{20,24},{24,28},{1,5},{5,9},{9,... | collective-permute-start | bytes 184328 | tf_op jit(solution)/shard_map/ppermute | solution.py:21
  8.1 2.6 %fusion.484 = (f32[]{:T(128)}, f32[31]{0:T(128)S(1)}, f32[]{:T(128)}, f32[31]{0:T(128)S(1)}, f32[]{:T(128)}, /*index=5*/f32[31]{0:T(128)S(1)}) fusion(f32[3,31]{1,0:T(4,128)S(1)} %multiply_reduce_fusion, f32[]{:T(128)} %bitcast.5, f32[]{:T(128)} %bitcast.11, f32[]{:T(128)} %bitcast.8), kind=kLoop, calls=%fused_computation.789 | loop fusion | flops 369 | bytes 768 | tf_op jit(solution)/shard_map/reduce_sum | solution.py:40
  13.6 0.7 fusion.500
  15.7 0.7 fusion.497
  16.4 0.7 fusion.495
  17.9 25.3 %fusion.318 = f32[16,64,128]{2,1,0:T(8,128)S(1)} fusion(f32[16,64,15]{2,1,0:T(8,128)S(1)} %collective-permute-done, f32[16,64,128]{2,1,0:T(8,128)S(1)} %copy-done, f32[16,64,143]{2,1,0:T(8,128)S(1)} %constant_dynamic-update-slice_fusion, f32[]{:T(128)} %bitcast.46, f32[]{:T(128)} %bitcast.45, f32[]{:T(128)} %bitcast.44, f32[]{:T(128)} %bitcast.43, ...), kind=kLoop, calls=%fused_computation.586 | loop fusion | flops 9961472 | bytes 8974460 | tf_op jit(solution)/shard_map/add | solution.py:50
  43.3 20.5 %fusion.408 = f32[16,64,128]{2,1,0:T(8,128)S(1)} fusion(f32[16,64,128]{2,1,0:T(8,128)S(1)} %fusion.318, f32[]{:T(128)} %bitcast.76, f32[]{:T(128)} %bitcast.75, f32[]{:T(128)} %bitcast.74, f32[]{:T(128)} %bitcast.73, f32[]{:T(128)} %bitcast.72, f32[]{:T(128)} %bitcast.71, f32[]{:T(128)} %bitcast.70, f32[]{:T(128)} %bitcast.69, f32[]{:T(128)} %bitcast.68, ...), kind=kLoop, calls=%fused_computation.676 | loop fusion | flops 7995392 | bytes 1048700 | tf_op jit(solution)/shard_map/add | solution.py:50
  63.9 3.4 %collective-permute-start.2 = (f32[16,15,128]{2,1,0:T(8,128)S(1)}, f32[16,15,128]{2,1,0:T(8,128)S(1)}, u32[]{:S(2)}, u32[]{:S(2)}) collective-permute-start(f32[16,15,128]{2,1,0:T(8,128)S(1)} %get-tuple-element.107), channel_id=1, source_target_pairs={{0,1},{1,2},{2,3},{4,5},{5,6},{6,7},{8,9},{9,10},{10,11},{12,13},{... | collective-permute-start | bytes 368648 | tf_op jit(solution)/shard_map/ppermute | solution.py:21
  67.3 1.3 collective-permute-start.3
  69.3 0.7 fusion.493
  70.0 0.9 collective-permute-done.2
  70.9 4.8 %collective-permute-done.3 = f32[16,15,128]{2,1,0:T(8,128)S(1)} collective-permute-done((f32[16,15,128]{2,1,0:T(8,128)S(1)}, f32[16,15,128]{2,1,0:T(8,128)S(1)}, u32[]{:S(2)}, u32[]{:S(2)}) %collective-permute-start.3) | collective-permute-done | bytes 122912 | tf_op jit(solution)/shard_map/ppermute | solution.py:23
  75.7 21.7 %fusion.130 = f32[16,64,128]{2,1,0:T(8,128)S(1)} fusion(f32[16,64,128]{2,1,0:T(8,128)S(1)} %copy-done.1, f32[16,64,128]{2,1,0:T(8,128)S(1)} %fusion.408, f32[16,15,128]{2,1,0:T(8,128)S(1)} %collective-permute-done.3, f32[16,15,128]{2,1,0:T(8,128)S(1)} %collective-permute-done.2, f32[]{:T(128)} %bitcast.106, f32[]{:T(128)} %bitcast.105, f32[]{:T(128)} %bitcast.104, ...), kind=kLoop, calls=%fused_computation.398 | loop fusion | flops 12058624 | bytes 1818748 | tf_op jit(solution)/shard_map/div | solution.py:108
  97.6 2.0 collective-permute-start.4
  99.6 3.5 %collective-permute-start.5 = (f32[16,64,15]{2,1,0:T(8,128)S(1)}, f32[16,64,15]{2,1,0:T(8,128)S(1)}, u32[]{:S(2)}, u32[]{:S(2)}) collective-permute-start(f32[16,64,15]{2,1,0:T(8,128)S(1)} %get-tuple-element.106), channel_id=1, source_target_pairs={{4,0},{8,4},{12,8},{16,12},{20,16},{24,20},{28,24},{5,1},{9,5},{13... | collective-permute-start | bytes 184328 | tf_op jit(solution)/shard_map/ppermute | solution.py:23
  103.9 4.2 %collective-permute-done.4 = f32[16,64,15]{2,1,0:T(8,128)S(1)} collective-permute-done((f32[16,64,15]{2,1,0:T(8,128)S(1)}, f32[16,64,15]{2,1,0:T(8,128)S(1)}, u32[]{:S(2)}, u32[]{:S(2)}) %collective-permute-start.4) | collective-permute-done | bytes 61472 | tf_op jit(solution)/shard_map/ppermute | solution.py:21
  108.1 1.8 collective-permute-done.5
  109.9 27.7 %fusion.216 = f32[16,64,128]{2,1,0:T(8,128)S(1)} fusion(f32[16,64,128]{2,1,0:T(8,128)S(1)} %fusion.130, f32[16,64,15]{2,1,0:T(8,128)S(1)} %collective-permute-done.5, f32[16,64,15]{2,1,0:T(8,128)S(1)} %collective-permute-done.4, f32[]{:T(128)} %bitcast.136, f32[]{:T(128)} %bitcast.135, f32[]{:T(128)} %bitcast.134, f32[]{:T(128)} %bitcast.133, f32[]{:T(128)} %bitcast.132, ...), kind=kLoop, calls=%fused_computation.484 | loop fusion | flops 11927552 | bytes 1171580 | tf_op jit(solution)/shard_map/add | solution.py:50
  137.5 20.2 %fusion.468 = f32[16,64,128]{2,1,0:T(8,128)S(1)} fusion(f32[16,64,128]{2,1,0:T(8,128)S(1)} %fusion.216, f32[]{:T(128)} %bitcast.166, f32[]{:T(128)} %bitcast.165, f32[]{:T(128)} %bitcast.164, f32[]{:T(128)} %bitcast.163, f32[]{:T(128)} %bitcast.162, f32[]{:T(128)} %bitcast.161, f32[]{:T(128)} %bitcast.160, f32[]{:T(128)} %bitcast.159, f32[]{:T(128)} %bitcast.158, ...), kind=kLoop, calls=%fused_computation.736 | loop fusion | flops 7995392 | bytes 1048700 | tf_op jit(solution)/shard_map/add | solution.py:50
  157.8 4.1 %collective-permute-start.6 = (f32[16,15,128]{2,1,0:T(8,128)S(1)}, f32[16,15,128]{2,1,0:T(8,128)S(1)}, u32[]{:S(2)}, u32[]{:S(2)}) collective-permute-start(f32[16,15,128]{2,1,0:T(8,128)S(1)} %get-tuple-element.103), channel_id=1, source_target_pairs={{0,1},{1,2},{2,3},{4,5},{5,6},{6,7},{8,9},{9,10},{10,11},{12,13},{... | collective-permute-start | bytes 368648 | tf_op jit(solution)/shard_map/ppermute | solution.py:21
  161.9 1.5 collective-permute-start.7
  164.1 0.7 fusion.491
  164.9 4.7 %collective-permute-done.7 = f32[16,15,128]{2,1,0:T(8,128)S(1)} collective-permute-done((f32[16,15,128]{2,1,0:T(8,128)S(1)}, f32[16,15,128]{2,1,0:T(8,128)S(1)}, u32[]{:S(2)}, u32[]{:S(2)}) %collective-permute-start.7) | collective-permute-done | bytes 122912 | tf_op jit(solution)/shard_map/ppermute | solution.py:23
  169.6 22.4 %fusion.43 = bf16[16,64,128]{2,1,0:T(8,128)(2,1)} fusion(f32[16,64,128]{2,1,0:T(8,128)S(1)} %copy-done, f32[16,64,128]{2,1,0:T(8,128)S(1)} %fusion.468, f32[16,15,128]{2,1,0:T(8,128)S(1)} %collective-permute-done.7, f32[16,15,128]{2,1,0:T(8,128)S(1)} %collective-permute-done.6, f32[]{:T(128)} %bitcast.196, f32[]{:T(128)} %bitcast.195, f32[]{:T(128)} %bitcast.194, ...), kind=kLoop, calls=%fused_computation.311 | loop fusion | flops 12189696 | bytes 1556604 | tf_op jit(solution)/shard_map/convert_element_type | solution.py:110
  192.0 3.4 %all-to-all-start = ((bf16[16,64,128]{2,1,0:T(8,128)(2,1)}), bf16[16,64,128]{2,1,0:T(8,128)(2,1)S(1)}, u32[]{:S(2)}, u32[]{:S(2)}) async-start(bf16[16,64,128]{2,1,0:T(8,128)(2,1)} %fusion.43), calls=%async_computation | async-start | bytes 524288 | tf_op jit(solution)/shard_map/all_to_all | solution.py:111
  195.4 6.0 %all-to-all-done = bf16[16,64,128]{2,1,0:T(8,128)(2,1)S(1)} async-done(((bf16[16,64,128]{2,1,0:T(8,128)(2,1)}), bf16[16,64,128]{2,1,0:T(8,128)(2,1)S(1)}, u32[]{:S(2)}, u32[]{:S(2)}) %all-to-all-start) | async-done | bytes 262176 | tf_op jit(solution)/shard_map/all_to_all | solution.py:111
  201.5 11.4 %while.13 = (s32[]{:T(128)}, f32[2,4,512,128]{3,2,1,0:T(8,128)S(1)}, s32[2]{0:T(128)S(1)}, bf16[4,256,128]{2,1,0:T(8,128)(2,1)S(1)}, s32[]{:T(128)}, /*index=5*/s32[1]{0:T(128)}) while((s32[]{:T(128)}, f32[2,4,512,128]{3,2,1,0:T(8,128)S(1)}, s32[2]{0:T(128)S(1)}, bf16[4,256,128]{2,1,0:T(8,128)(2,1)S(1)}, s32[]{:T(128)}, ...), condition=%wide.region_6.7_spmd, body=%wide.region_5.6_spmd.sunk | while | flops 139854592 | bytes 1316965 | solution.py:98
  202.8 4.4 %fusion.510 = f32[2,4,512,128]{3,2,1,0:T(8,128)S(1)} fusion(f32[2,4,512,128]{3,2,1,0:T(8,128)S(1)} %get-tuple-element.342, s32[]{:T(128)} %get-tuple-element.341, bf16[4,256,128]{2,1,0:T(8,128)(2,1)S(1)} %get-tuple-element.350, s32[256]{0:T(256)S(1)} %iota_multiply_fusion.2, s32[512]{0:T(512)S(1)} %iota_add_fusion.2), kind=kOutput, calls=%fused_computation.1.clone.1 | convolution fusion | flops 139853824 | bytes 1313796 | tf_op jit(solution)/shard_map/while/body/eval_jaxpr/ep,hps->hes/dot_general | solution.py:94
  208.5 4.4 %fusion.510 = f32[2,4,512,128]{3,2,1,0:T(8,128)S(1)} fusion(f32[2,4,512,128]{3,2,1,0:T(8,128)S(1)} %get-tuple-element.342, s32[]{:T(128)} %get-tuple-element.341, bf16[4,256,128]{2,1,0:T(8,128)(2,1)S(1)} %get-tuple-element.350, s32[256]{0:T(256)S(1)} %iota_multiply_fusion.2, s32[512]{0:T(512)S(1)} %iota_add_fusion.2), kind=kOutput, calls=%fused_computation.1.clone.1 | convolution fusion | flops 139853824 | bytes 1313796 | tf_op jit(solution)/shard_map/while/body/eval_jaxpr/ep,hps->hes/dot_general | solution.py:94
  212.9 1.5 copy.7
  (42 shorter events, 9.6 us)
Async XLA Ops:
  0.0 12.8 %copy-start = (f32[16,64,128]{2,1,0:T(8,128)S(1)}, f32[16,64,128]{2,1,0:T(8,128)}, u32[]{:S(2)}) copy-start(f32[16,64,128]{2,1,0:T(8,128)} %param.10) | copy-start | bytes 1572868
  0.0 7.2 %copy-start.3 = (s32[6,3]{0,1:T(4,128)S(1)}, s32[6,3]{0,1:T(4,128)}, u32[]{:S(2)}) copy-start(s32[6,3]{0,1:T(4,128)} %param.9) | copy-start | bytes 220
  0.0 8.0 %copy-start.2 = (f32[6,3,31]{2,1,0:T(4,128)S(1)}, f32[6,3,31]{2,1,0:T(4,128)}, u32[]{:S(2)}) copy-start(f32[6,3,31]{2,1,0:T(4,128)} %param.8) | copy-start | bytes 6700
  2.2 15.6 %collective-permute-start.1 = (f32[16,64,15]{2,1,0:T(8,128)}, f32[16,64,15]{2,1,0:T(8,128)S(1)}, u32[]{:S(2)}, u32[]{:S(2)}) collective-permute-start(f32[16,64,15]{2,1,0:T(8,128)} %get-tuple-element.109), channel_id=1, source_target_pairs={{4,0},{8,4},{12,8},{16,12},{20,16},{24,20},{28,24},{5,1},{9,5},{13... | collective-permute-start | bytes 184328 | tf_op jit(solution)/shard_map/ppermute | solution.py:23
  4.1 13.8 %collective-permute-start = (f32[16,64,15]{2,1,0:T(8,128)S(1)}, f32[16,64,15]{2,1,0:T(8,128)S(1)}, u32[]{:S(2)}, u32[]{:S(2)}) collective-permute-start(f32[16,64,15]{2,1,0:T(8,128)S(1)} %get-tuple-element.110), channel_id=1, source_target_pairs={{0,4},{4,8},{8,12},{12,16},{16,20},{20,24},{24,28},{1,5},{5,9},{9,... | collective-permute-start | bytes 184328 | tf_op jit(solution)/shard_map/ppermute | solution.py:21
  43.3 32.4 %copy-start.1 = (f32[16,64,128]{2,1,0:T(8,128)S(1)}, f32[16,64,128]{2,1,0:T(8,128)}, u32[]{:S(2)}) copy-start(f32[16,64,128]{2,1,0:T(8,128)} %param.11) | copy-start | bytes 1572868
  63.9 7.1 %collective-permute-start.2 = (f32[16,15,128]{2,1,0:T(8,128)S(1)}, f32[16,15,128]{2,1,0:T(8,128)S(1)}, u32[]{:S(2)}, u32[]{:S(2)}) collective-permute-start(f32[16,15,128]{2,1,0:T(8,128)S(1)} %get-tuple-element.107), channel_id=1, source_target_pairs={{0,1},{1,2},{2,3},{4,5},{5,6},{6,7},{8,9},{9,10},{10,11},{12,13},{... | collective-permute-start | bytes 368648 | tf_op jit(solution)/shard_map/ppermute | solution.py:21
  67.3 8.4 %collective-permute-start.3 = (f32[16,15,128]{2,1,0:T(8,128)S(1)}, f32[16,15,128]{2,1,0:T(8,128)S(1)}, u32[]{:S(2)}, u32[]{:S(2)}) collective-permute-start(f32[16,15,128]{2,1,0:T(8,128)S(1)} %get-tuple-element.108), channel_id=1, source_target_pairs={{1,0},{2,1},{3,2},{5,4},{6,5},{7,6},{9,8},{10,9},{11,10},{13,12},{... | collective-permute-start | bytes 368648 | tf_op jit(solution)/shard_map/ppermute | solution.py:23
  97.6 10.5 %collective-permute-start.4 = (f32[16,64,15]{2,1,0:T(8,128)S(1)}, f32[16,64,15]{2,1,0:T(8,128)S(1)}, u32[]{:S(2)}, u32[]{:S(2)}) collective-permute-start(f32[16,64,15]{2,1,0:T(8,128)S(1)} %get-tuple-element.105), channel_id=1, source_target_pairs={{0,4},{4,8},{8,12},{12,16},{16,20},{20,24},{24,28},{1,5},{5,9},{9,... | collective-permute-start | bytes 184328 | tf_op jit(solution)/shard_map/ppermute | solution.py:21
  99.6 10.2 %collective-permute-start.5 = (f32[16,64,15]{2,1,0:T(8,128)S(1)}, f32[16,64,15]{2,1,0:T(8,128)S(1)}, u32[]{:S(2)}, u32[]{:S(2)}) collective-permute-start(f32[16,64,15]{2,1,0:T(8,128)S(1)} %get-tuple-element.106), channel_id=1, source_target_pairs={{4,0},{8,4},{12,8},{16,12},{20,16},{24,20},{28,24},{5,1},{9,5},{13... | collective-permute-start | bytes 184328 | tf_op jit(solution)/shard_map/ppermute | solution.py:23
  157.8 7.1 %collective-permute-start.6 = (f32[16,15,128]{2,1,0:T(8,128)S(1)}, f32[16,15,128]{2,1,0:T(8,128)S(1)}, u32[]{:S(2)}, u32[]{:S(2)}) collective-permute-start(f32[16,15,128]{2,1,0:T(8,128)S(1)} %get-tuple-element.103), channel_id=1, source_target_pairs={{0,1},{1,2},{2,3},{4,5},{5,6},{6,7},{8,9},{9,10},{10,11},{12,13},{... | collective-permute-start | bytes 368648 | tf_op jit(solution)/shard_map/ppermute | solution.py:21
  161.9 7.7 %collective-permute-start.7 = (f32[16,15,128]{2,1,0:T(8,128)S(1)}, f32[16,15,128]{2,1,0:T(8,128)S(1)}, u32[]{:S(2)}, u32[]{:S(2)}) collective-permute-start(f32[16,15,128]{2,1,0:T(8,128)S(1)} %get-tuple-element.104), channel_id=1, source_target_pairs={{1,0},{2,1},{3,2},{5,4},{6,5},{7,6},{9,8},{10,9},{11,10},{13,12},{... | collective-permute-start | bytes 368648 | tf_op jit(solution)/shard_map/ppermute | solution.py:23
  192.0 9.5 %all-to-all-start = ((bf16[16,64,128]{2,1,0:T(8,128)(2,1)}), bf16[16,64,128]{2,1,0:T(8,128)(2,1)S(1)}, u32[]{:S(2)}, u32[]{:S(2)}) async-start(bf16[16,64,128]{2,1,0:T(8,128)(2,1)} %fusion.43), calls=%async_computation | async-start | bytes 524288 | tf_op jit(solution)/shard_map/all_to_all | solution.py:111
where the time goes:
time: 216 us; the launch traced here: 214 us
  other arithmetic  143 us (66%)
  starting transfers between devices  23.6 us (11%)
  waiting for transfers between devices  22.4 us (10%)
  local copies, waits for them, and re-layouts  14.7 us (7%)
  matrix products  8.88 us (4%)
    add x4, other arithmetic, smear_valid(): total + kernel[tap_index] * lax.slice_in_dim(padded, tap_index, tap_index...  93.8 us
    convert_element_type x1, other arithmetic, on_device(): rounded = (estimate * correction).astype(jnp.bfloat16)  22.4 us
    div x1, other arithmetic, on_device(): quotient = measured / blurred  21.7 us
    ppermute x4, starting transfers between devices, extended(): lax.ppermute(tail, axis, [(i, (i + 1) % count) for i in range(ends)])  11.9 us
    ppermute x4, waiting for transfers between devices, extended(): lax.ppermute(head, axis, [((i + 1) % count, i) for i in range(ends)])  11.2 us
    dot_general x2, matrix products, block_out(): jnp.einsum('ep,hps->hes', slab_lookup_table, depth_columns, preferred_ele...  8.88 us
    slice x12, local copies, waits for them, and re-layouts, smear_valid(): kernel[tap_index]  8.54 us
    ppermute x4, starting transfers between devices, extended(): lax.ppermute(head, axis, [((i + 1) % count, i) for i in range(ends)])  8.21 us
  transfers between devices with their start and end apart: 9, of which 7 were waited for; matrix products, arithmetic and copies ran while one was open for 7% of the time, Pallas kernels for 0%

commit v1 on v0

v1 whole, which is shorter than its diff:
```python
import functools

import jax
import jax.numpy as jnp
from jax import lax
from jax.experimental import pallas as pl
from jax.experimental.pallas import tpu as pltpu
from jax.sharding import PartitionSpec as P

HALF = 15
TAPS = 31
UP = 4
PAD = 16
BF = jnp.bfloat16
F32 = jnp.float32
MESH = pl.DeviceIdType.MESH
AROUND = [(dx, dz) for dz in (-1, 1, 0) for dx in (0, -1, 1) if (dx, dz) != (0, 0)]


def dot(a, b):
    return jnp.dot(a, b, preferred_element_type=F32)


def lanes_of(shape):
    return lax.broadcasted_iota(jnp.int32, shape, 1)


def rows_of(shape):
    return lax.broadcasted_iota(jnp.int32, shape, 0)


def tap_row(taps_ref, view, extents_ref, axis_id, width, spread, flip):
    lane = lanes_of((8, width))
    row = jnp.zeros((8, width), F32)
    for t in range(TAPS):
        spot = (TAPS - 1 - t if flip else t) * spread
        row = jnp.where(lane == spot, taps_ref[view, axis_id, t], row)
    keep = jnp.abs(lane - HALF * spread) <= extents_ref[view, axis_id] * spread
    row = jnp.where(keep, row, 0.0)
    return row / jnp.sum(row, axis=1, keepdims=True)


def slanted(row, count, shift):
    width = row.shape[1]
    tall = jnp.broadcast_to(row[0:1], (count, width))
    return pltpu.roll(tall, shift % width, 1, stride=1, stride_axis=0)


def make_matrices(taps_ref, view, extents_ref, flip, mz, too, wide, ky, ny, nz, nx):
    group = nx // PAD
    mz[...] = slanted(tap_row(taps_ref, view, extents_ref, 2, nx, 1, flip), nz, 1)[
        :, : nz + 2 * PAD
    ].astype(BF)
    ring = slanted(tap_row(taps_ref, view, extents_ref, 0, nx, 1, not flip), nx, -HALF)
    lane, row = lanes_of((nx, nx)), rows_of((nx, nx))
    too[...] = jnp.where(jnp.abs(lane - row) <= HALF, ring, 0.0).astype(BF)
    edge = lanes_of((PAD, nx))
    from_left = jnp.where(edge < nx // 2, ring[nx - PAD :], 0.0).astype(BF)
    from_right = jnp.where(edge >= nx // 2, ring[:PAD], 0.0).astype(BF)
    wide[...] = jnp.zeros(wide.shape, BF)
    for j in range(group):
        wide[j * PAD : (j + 1) * PAD, j * nx : (j + 1) * nx] = from_left
        wide[nx + j * PAD : nx + (j + 1) * PAD, j * nx : (j + 1) * nx] = from_right
    sub = 8
    long = tap_row(taps_ref, view, extents_ref, 1, 2 * ny * sub, sub, flip)
    ky[...] = slanted(long, ny * sub, -HALF * sub)[:, : ny * sub].astype(BF)


def make_table(table, length):
    shape = (PAD, length)
    offset = jnp.bitwise_and(rows_of(shape) - UP * lanes_of(shape), UP * length - 1)
    sine = jnp.sin(jnp.pi * jnp.bitwise_and(offset, 2 * UP - 1).astype(F32) / UP)
    angle = jnp.pi * offset.astype(F32) / (UP * length)
    on_grid = jnp.bitwise_and(offset, UP - 1) == 0
    below = jnp.where(on_grid, 1.0, length * jnp.sin(angle) / jnp.where(on_grid, 1.0, jnp.cos(angle)))
    first = jnp.where(on_grid, jnp.where(offset == 0, 1.0, 0.0), sine / below)

    def fill(j, carry):
        table[pl.ds(pl.multiple_of(j * PAD, PAD), PAD), :] = pltpu.roll(
            first, j * (PAD // UP), 1
        ).astype(BF)
        return carry

    lax.fori_loop(0, UP * length // PAD, fill, 0)


def pack_edges(volume, packed, ny, nz, nx):
    group = nx // PAD
    lane = lanes_of((nz, nx)) // PAD
    for g in range(ny // group):
        left = right = None
        for j in range(group):
            plane = volume(g * group + j)
            a = pltpu.roll(plane, (j * PAD) % nx, 1) if j else plane
            s = (j * PAD - (nx - PAD)) % nx
            b = pltpu.roll(plane, s, 1) if s else plane
            left = a if left is None else jnp.where(lane == j, a, left)
            right = b if right is None else jnp.where(lane == j, b, right)
        packed[0, g] = left.astype(BF)
        packed[1, g] = right.astype(BF)


def blur(ext, side, mz, too, wide, ky, held, ny, nz, nx):
    group = nx // PAD
    m = mz[...]
    s = [
        jnp.concatenate([dot(m, side[q, g]) for q in range(2)], axis=1).astype(BF)
        for g in range(ny // group)
    ]
    vs = [dot(part, wide[...]) for part in s]
    for y in range(ny):
        u = dot(m, ext[y]).astype(BF)
        g, j = divmod(y, group)
        held[y] = dot(u, too[...]) + vs[g][:, j * nx : (j + 1) * nx]
    for k in range(nz // 8):
        a = held[:, k * 8 : (k + 1) * 8, :].reshape(ny * 8, nx).astype(BF)
        yield k, dot(ky[...], a).reshape(ny, 8, nx)


def kernel(
    ngx, ngz,
    view_ref, taps_ref, extents_ref, est_ref, mea_ref,
    out_ref, table_ref,
    ext, side, packed, gathered, leaving, held, quot,
    mz, too, wide, ky,
    send_sem, recv_sem, all_send, all_recv,
):
    ny, nz, nx = est_ref.shape
    planes = ny // ngz
    gx, gz = lax.axis_index("gx"), lax.axis_index("gz")
    has_x = {-1: gx > 0, 0: True, 1: gx < ngx - 1}
    has_z = {-1: gz > 0, 0: True, 1: gz < ngz - 1}

    def there(dx, dz):
        if dx == 0:
            return has_z[dz]
        if dz == 0:
            return has_x[dx]
        return jnp.logical_and(has_x[dx], has_z[dz])

    barrier = pltpu.get_barrier_semaphore()
    total = ngz - 1
    for d in range(1, ngz):
        pl.semaphore_signal(
            barrier, inc=1, device_id=(gx, lax.rem(gz + d, ngz)), device_id_type=MESH
        )
    for dx, dz in AROUND:
        if dx == 0:
            continue
        here = there(dx, dz)
        total = total + jnp.where(here, 1, 0)

        @pl.when(here)
        def _(dx=dx, dz=dz):
            pl.semaphore_signal(
                barrier, inc=1, device_id=(gx + dx, gz + dz), device_id_type=MESH
            )

    def landing(r, dx, dz):
        first, count = {-1: (0, PAD), 0: (PAD, nz), 1: (PAD + nz, PAD)}[dz]
        rows = pl.ds(first, count)
        if dx == 0:
            return ext.at[r, :, rows, :]
        return side.at[r, 0 if dx < 0 else 1, :, rows, :]

    def copy(r, dx, dz):
        first, count = {-1: (0, PAD), 0: (0, nz), 1: (nz - PAD, PAD)}[dz]
        if dx == 0:
            src = ext.at[r, :, pl.ds(PAD + first, count), :]
        else:
            src = packed.at[r, 0 if dx < 0 else 1, :, pl.ds(first, count), :]
        return pltpu.make_async_remote_copy(
            src_ref=src,
            dst_ref=landing(r, -dx, -dz),
            send_sem=send_sem.at[r, AROUND.index((dx, dz))],
            recv_sem=recv_sem.at[r, AROUND.index((-dx, -dz))],
            device_id=(gx + dx, gz + dz),
            device_id_type=MESH,
        )

    def arrival(r, dx, dz):
        first, count = {-1: (0, PAD), 0: (0, nz), 1: (nz - PAD, PAD)}[dz]
        dst = landing(r, dx, dz)
        return pltpu.make_async_remote_copy(
            src_ref=dst,
            dst_ref=dst,
            send_sem=send_sem.at[r, AROUND.index((dx, dz))],
            recv_sem=recv_sem.at[r, AROUND.index((dx, dz))],
            device_id=(gx + dx, gz + dz),
            device_id_type=MESH,
        )

    def clear(r):
        for dx, dz in AROUND:
            @pl.when(jnp.logical_not(there(dx, dz)))
            def _(dx=dx, dz=dz):
                spot = landing(r, dx, dz)
                spot[...] = jnp.zeros(spot.shape, BF)

    def send(r):
        for dx, dz in AROUND:
            @pl.when(there(dx, dz))
            def _(dx=dx, dz=dz):
                copy(r, dx, dz).start()

    def receive(r):
        for dx, dz in AROUND:
            @pl.when(there(dx, dz))
            def _(dx=dx, dz=dz):
                arrival(r, dx, dz).wait_recv()

    def sent(r):
        for dx, dz in AROUND:
            @pl.when(there(dx, dz))
            def _(dx=dx, dz=dz):
                copy(r, dx, dz).wait_send()

    ext[0, :, PAD : PAD + nz, :] = est_ref[...].astype(BF)
    pack_edges(lambda y: est_ref[y], packed.at[0], ny, nz, nx)
    pl.semaphore_wait(barrier, total)
    send(0)

    view = view_ref[0]
    for flip in range(2):
        make_matrices(
            taps_ref, view, extents_ref, bool(flip),
            mz.at[flip], too.at[flip], wide.at[flip], ky.at[flip], ny, nz, nx,
        )
    clear(0)
    clear(1)
    make_table(table_ref, nz * ngz)
    receive(0)
    for k, value in blur(ext.at[0], side.at[0], mz[0], too[0], wide[0], ky[0], held, ny, nz, nx):
        rows = pl.ds(k * 8, 8)
        quot[:, rows, :] = mea_ref[:, rows, :] / value
    ext[1, :, PAD : PAD + nz, :] = quot[...].astype(BF)
    pack_edges(lambda y: quot[y], packed.at[1], ny, nz, nx)
    send(1)
    receive(1)
    for k, value in blur(ext.at[1], side.at[1], mz[1], too[1], wide[1], ky[1], held, ny, nz, nx):
        rows = pl.ds(k * 8, 8)
        quot[:, rows, :] = est_ref[:, rows, :] * value
    leaving[...] = quot[...].astype(BF)

    def exchange(d):
        to = lax.rem(gz + d, ngz)
        return pltpu.make_async_remote_copy(
            src_ref=leaving.at[pl.ds(to * planes, planes)],
            dst_ref=gathered.at[:, pl.ds(pl.multiple_of(gz * nz, nz), nz), :],
            send_sem=all_send.at[d],
            recv_sem=all_recv.at[d],
            device_id=(gx, to),
            device_id_type=MESH,
        )

    for d in range(1, ngz):
        exchange(d).start()
    mine = pl.ds(pl.multiple_of(gz * nz, nz), nz)
    gathered[:, mine, :] = leaving[pl.ds(gz * planes, planes)]
    for d in range(1, ngz):
        exchange(d).wait_recv()
    out_ref[...] = gathered[...]
    sent(0)
    sent(1)
    for d in range(1, ngz):
        exchange(d).wait_send()


def upsample_kernel(table_ref, lines_ref, out_ref):
    out_ref[0] = dot(table_ref[...], lines_ref[0])


def on_device(ngx, ngz, view_index, psf_taps, extents, estimate, measured):
    ny, nz, nx = estimate.shape
    planes, lines = ny // ngz, nz * ngz
    group = nx // PAD
    smem = pl.BlockSpec(memory_space=pltpu.SMEM)
    vmem = pl.BlockSpec(memory_space=pltpu.VMEM)
    gathered, table = pl.pallas_call(
        functools.partial(kernel, ngx, ngz),
        out_shape=[
            jax.ShapeDtypeStruct((planes, lines, nx), BF),
            jax.ShapeDtypeStruct((UP * lines, lines), BF),
        ],
        in_specs=[smem, smem, smem, vmem, vmem],
        out_specs=[vmem, vmem],
        scratch_shapes=[
            pltpu.VMEM((2, ny, nz + 2 * PAD, nx), BF),
            pltpu.VMEM((2, 2, ny // group, nz + 2 * PAD, nx), BF),
            pltpu.VMEM((2, 2, ny // group, nz, nx), BF),
            pltpu.VMEM((planes, lines, nx), BF),
            pltpu.VMEM((ny, nz, nx), BF),
            pltpu.VMEM((ny, nz, nx), F32),
            pltpu.VMEM((ny, nz, nx), F32),
            pltpu.VMEM((2, nz, nz + 2 * PAD), BF),
            pltpu.VMEM((2, nx, nx), BF),
            pltpu.VMEM((2, 2 * nx, group * nx), BF),
            pltpu.VMEM((2, ny * 8, ny * 8), BF),
            pltpu.SemaphoreType.DMA((2, 8)),
            pltpu.SemaphoreType.DMA((2, 8)),
            pltpu.SemaphoreType.DMA((ngz,)),
            pltpu.SemaphoreType.DMA((ngz,)),
        ],
        compiler_params=pltpu.CompilerParams(collective_id=0, has_side_effects=True),
    )(view_index, psf_taps, extents, estimate, measured)
    return pl.pallas_call(
        upsample_kernel,
        grid=(planes,),
        out_shape=jax.ShapeDtypeStruct((planes, UP * lines, nx), F32),
        in_specs=[
            pl.BlockSpec((UP * lines, lines), lambda y: (0, 0)),
            pl.BlockSpec((1, lines, nx), lambda y: (y, 0, 0)),
        ],
        out_specs=pl.BlockSpec((1, UP * lines, nx), lambda y: (y, 0, 0)),
    )(table, gathered)


def solution(mesh):
    return jax.shard_map(
        functools.partial(on_device, mesh.shape["gx"], mesh.shape["gz"]),
        mesh=mesh,
        in_specs=(P(), P(), P(), P(None, "gz", "gx"), P(None, "gz", "gx")),
        out_specs=P("gz", None, "gx"),
        check_vma=False,
    )
```

time: 216 us -> 32 us (0.15)
  the two profiles are of different devices: /device:TPU:8 before, /device:TPU:0 now
where the time goes in v1:
time: 32 us; the launch traced here: 31.7 us
  Pallas kernels  29.6 us (92%)
  local copies, waits for them, and re-layouts  1.35 us (4%)
  between operations  0.66 us (2%)
    pallas_call x1, Pallas kernels, on_device(): pl.pallas_call(functools.partial(kernel, ngx, ngz), out_shape=[jax.ShapeD...  25.5 us
    pallas_call x1, Pallas kernels, on_device(): pl.pallas_call(upsample_kernel, grid=(planes,), out_shape=jax.ShapeDtypeS...  4.12 us
    unnamed x1, local copies, waits for them, and re-layouts  1.35 us

profile of v1, /device:TPU:0, one launch (start us, length us, event | category | flops | bytes accessed | tf_op | source)
XLA Modules:
  0.0 31.7 jit_solution(2591692483912895179)
XLA Ops:
  0.7 1.4 %copy.6.extents_ref = s32[6,3]{1,0:T(8,128)} copy(s32[6,3]{0,1:T(4,128)} %param.7) | data formatting | bytes 144 | tf_op args[2]
  2.0 25.5 %shard_map.55 = (bf16[4,256,128]{2,1,0:T(8,128)(2,1)}, bf16[1024,256]{1,0:T(8,128)(2,1)}) custom-call(s32[1]{0:T(128)S(6)} %copy.7.view_ref, f32[6,3,31]{2,1,0:T(4,128)} %taps_ref.1, s32[6,3]{1,0:T(8,128)} %copy.6.extents_ref, f32[16,64,128]{2,1,0:T(8,128)} %est_ref.1, f32[16,64,128]{2,1,0:T(8,128)} %mea_ref.1), custom_call_target="tpu_custom_call" | custom-call | tf_op jit(solution)/shard_map/pallas_call | solution.py:279
  27.5 4.1 %shard_map.56 = f32[4,1024,128]{2,1,0:T(8,128)} custom-call(bf16[1024,256]{1,0:T(8,128)(2,1)} %get-tuple-element.7.table_ref, bf16[4,256,128]{2,1,0:T(8,128)(2,1)} %get-tuple-element.8.lines_ref), custom_call_target="tpu_custom_call" | custom-call | tf_op jit(solution)/shard_map/pallas_call | solution.py:306

commit v2 on v1

--- a/solution.py
+++ b/solution.py
@@ -35,7 +35,7 @@
     for t in range(TAPS):
         spot = (TAPS - 1 - t if flip else t) * spread
         row = jnp.where(lane == spot, taps_ref[view, axis_id, t], row)
-    keep = jnp.abs(lane - HALF * spread) <= extents_ref[view, axis_id] * spread
+    keep = jnp.abs(lane - HALF * spread) <= extents_ref[axis_id, view] * spread
     row = jnp.where(keep, row, 0.0)
     return row / jnp.sum(row, axis=1, keepdims=True)
 
@@ -75,13 +75,9 @@
     below = jnp.where(on_grid, 1.0, length * jnp.sin(angle) / jnp.where(on_grid, 1.0, jnp.cos(angle)))
     first = jnp.where(on_grid, jnp.where(offset == 0, 1.0, 0.0), sine / below)
 
-    def fill(j, carry):
-        table[pl.ds(pl.multiple_of(j * PAD, PAD), PAD), :] = pltpu.roll(
-            first, j * (PAD // UP), 1
-        ).astype(BF)
-        return carry
-
-    lax.fori_loop(0, UP * length // PAD, fill, 0)
+    for j in range(UP * length // PAD):
+        moved = pltpu.roll(first, j * (PAD // UP), 1) if j else first
+        table[j * PAD : (j + 1) * PAD, :] = moved.astype(BF)
 
 
 def pack_edges(volume, packed, ny, nz, nx):
@@ -100,31 +96,38 @@
         packed[1, g] = right.astype(BF)
 
 
-def blur(ext, side, mz, too, wide, ky, held, ny, nz, nx):
+def blur_rows(start, count, ext, side, mz, too, wide, ky, held, ny, nx):
     group = nx // PAD
-    m = mz[...]
+    reach = count + 2 * PAD
+    m = mz[0:count, 0:reach]
+    near = pl.ds(start, reach)
     s = [
-        jnp.concatenate([dot(m, side[q, g]) for q in range(2)], axis=1).astype(BF)
+        jnp.concatenate([dot(m, side[q, g, near, :]) for q in range(2)], axis=1).astype(BF)
         for g in range(ny // group)
     ]
     vs = [dot(part, wide[...]) for part in s]
     for y in range(ny):
-        u = dot(m, ext[y]).astype(BF)
+        u = dot(m, ext[y, near, :]).astype(BF)
         g, j = divmod(y, group)
-        held[y] = dot(u, too[...]) + vs[g][:, j * nx : (j + 1) * nx]
-    for k in range(nz // 8):
+        held[y, pl.ds(start, count), :] = dot(u, too[...]) + vs[g][:, j * nx : (j + 1) * nx]
+    for k in range(start // 8, (start + count) // 8):
         a = held[:, k * 8 : (k + 1) * 8, :].reshape(ny * 8, nx).astype(BF)
-        yield k, dot(ky[...], a).reshape(ny, 8, nx)
+        yield pl.ds(k * 8, 8), dot(ky[...], a).reshape(ny, 8, nx)
 
 
 def kernel(
     ngx, ngz,
-    view_ref, taps_ref, extents_ref, est_ref, mea_ref,
-    out_ref, table_ref,
+    view_ref, taps_ref, extents_ref, est_hbm, mea_hbm,
+    out_ref,
+    est_ref, mea_ref, table_ref,
     ext, side, packed, gathered, leaving, held, quot,
     mz, too, wide, ky,
-    send_sem, recv_sem, all_send, all_recv,
+    send_sem, recv_sem, all_send, all_recv, load_sem,
 ):
+    load_est = pltpu.make_async_copy(est_hbm, est_ref, load_sem.at[0])
+    load_mea = pltpu.make_async_copy(mea_hbm, mea_ref, load_sem.at[1])
+    load_est.start()
+    load_mea.start()
     ny, nz, nx = est_ref.shape
     planes = ny // ngz
     gx, gz = lax.axis_index("gx"), lax.axis_index("gz")
@@ -197,14 +200,14 @@
                 spot = landing(r, dx, dz)
                 spot[...] = jnp.zeros(spot.shape, BF)
 
-    def send(r):
-        for dx, dz in AROUND:
+    def send(r, which):
+        for dx, dz in which:
             @pl.when(there(dx, dz))
             def _(dx=dx, dz=dz):
                 copy(r, dx, dz).start()
 
-    def receive(r):
-        for dx, dz in AROUND:
+    def receive(r, which):
+        for dx, dz in which:
             @pl.when(there(dx, dz))
             def _(dx=dx, dz=dz):
                 arrival(r, dx, dz).wait_recv()
@@ -215,11 +218,54 @@
             def _(dx=dx, dz=dz):
                 copy(r, dx, dz).wait_send()
 
+    above = [(0, -1), (0, 1)]
+    sideways = [(-1, 0), (1, 0)]
+    corners = [d for d in AROUND if d[0] and d[1]]
+    middle = [(PAD, nz - 2 * PAD)]
+    ends = [(0, PAD), (nz - PAD, PAD)]
+    parts = middle + ends
+
+    def exchange(d, part):
+        to = lax.rem(gz + d, ngz)
+        first, count = parts[part]
+        there_rows = pl.ds(pl.multiple_of(gz * nz + first, PAD), count)
+        return pltpu.make_async_remote_copy(
+            src_ref=leaving.at[pl.ds(to * planes, planes), pl.ds(first, count), :],
+            dst_ref=gathered.at[:, there_rows, :],
+            send_sem=all_send.at[d, part],
+            recv_sem=all_recv.at[d, part],
+            device_id=(gx, to),
+            device_id_type=MESH,
+        )
+
+    def blurred(r, blocks):
+        for first, count in blocks:
+            yield from blur_rows(
+                first, count, ext.at[r], side.at[r],
+                mz.at[r], too.at[r], wide.at[r], ky.at[r], held, ny, nx,
+            )
+
+    def quotients(blocks):
+        for rows, value in blurred(0, blocks):
+            quot[:, rows, :] = mea_ref[:, rows, :] / value
+        for first, count in blocks:
+            ext[1, :, PAD + first : PAD + first + count, :] = quot[
+                :, first : first + count, :
+            ].astype(BF)
+
+    def products(blocks):
+        for rows, value in blurred(1, blocks):
+            held[:, rows, :] = est_ref[:, rows, :] * value
+        for first, count in blocks:
+            rows = slice(first, first + count)
+            leaving[:, rows, :] = held[:, rows, :].astype(BF)
+
+    load_est.wait()
     ext[0, :, PAD : PAD + nz, :] = est_ref[...].astype(BF)
+    pl.semaphore_wait(barrier, total)
+    send(0, above)
     pack_edges(lambda y: est_ref[y], packed.at[0], ny, nz, nx)
-    pl.semaphore_wait(barrier, total)
-    send(0)
-
+    send(0, corners + sideways)
     view = view_ref[0]
     for flip in range(2):
         make_matrices(
@@ -228,46 +274,41 @@
         )
     clear(0)
     clear(1)
+    load_mea.wait()
+    receive(0, sideways)
+    quotients(middle)
+    receive(0, above + corners)
+    quotients(ends)
+    send(1, above)
+    pack_edges(lambda y: quot[y], packed.at[1], ny, nz, nx)
+    send(1, corners + sideways)
     make_table(table_ref, nz * ngz)
-    receive(0)
-    for k, value in blur(ext.at[0], side.at[0], mz[0], too[0], wide[0], ky[0], held, ny, nz, nx):
-        rows = pl.ds(k * 8, 8)
-        quot[:, rows, :] = mea_ref[:, rows, :] / value
-    ext[1, :, PAD : PAD + nz, :] = quot[...].astype(BF)
-    pack_edges(lambda y: quot[y], packed.at[1], ny, nz, nx)
-    send(1)
-    receive(1)
-    for k, value in blur(ext.at[1], side.at[1], mz[1], too[1], wide[1], ky[1], held, ny, nz, nx):
-        rows = pl.ds(k * 8, 8)
-        quot[:, rows, :] = est_ref[:, rows, :] * value
-    leaving[...] = quot[...].astype(BF)
-
-    def exchange(d):
-        to = lax.rem(gz + d, ngz)
-        return pltpu.make_async_remote_copy(
-            src_ref=leaving.at[pl.ds(to * planes, planes)],
-            dst_ref=gathered.at[:, pl.ds(pl.multiple_of(gz * nz, nz), nz), :],
-            send_sem=all_send.at[d],
-            recv_sem=all_recv.at[d],
-            device_id=(gx, to),
-            device_id_type=MESH,
-        )
-
-    for d in range(1, ngz):
-        exchange(d).start()
+    receive(1, sideways)
+    products(middle)
+    for d in range(1, ngz):
+        exchange(d, 0).start()
+    receive(1, above + corners)
+    products(ends)
+    for d in range(1, ngz):
+        for part in (1, 2):
+            exchange(d, part).start()
     mine = pl.ds(pl.multiple_of(gz * nz, nz), nz)
     gathered[:, mine, :] = leaving[pl.ds(gz * planes, planes)]
     for d in range(1, ngz):
-        exchange(d).wait_recv()
-    out_ref[...] = gathered[...]
+        for part in range(3):
+            exchange(d, part).wait_recv()
+    lines = jnp.concatenate([gathered[y] for y in range(planes)], axis=1)
+    step = nz * ngz
+    for b in range(UP):
+        rows = slice(b * step, (b + 1) * step)
+        whole = dot(table_ref[rows, :], lines)
+        for y in range(planes):
+            out_ref[y, rows, :] = whole[:, y * nx : (y + 1) * nx]
     sent(0)
     sent(1)
     for d in range(1, ngz):
-        exchange(d).wait_send()
-
-
-def upsample_kernel(table_ref, lines_ref, out_ref):
-    out_ref[0] = dot(table_ref[...], lines_ref[0])
+        for part in range(3):
+            exchange(d, part).wait_send()
 
 
 def on_device(ngx, ngz, view_index, psf_taps, extents, estimate, measured):
@@ -276,15 +317,16 @@
     group = nx // PAD
     smem = pl.BlockSpec(memory_space=pltpu.SMEM)
     vmem = pl.BlockSpec(memory_space=pltpu.VMEM)
-    gathered, table = pl.pallas_call(
+    anywhere = pl.BlockSpec(memory_space=pl.ANY)
+    return pl.pallas_call(
         functools.partial(kernel, ngx, ngz),
-        out_shape=[
-            jax.ShapeDtypeStruct((planes, lines, nx), BF),
-            jax.ShapeDtypeStruct((UP * lines, lines), BF),
-        ],
-        in_specs=[smem, smem, smem, vmem, vmem],
-        out_specs=[vmem, vmem],
+        out_shape=pltpu.VMEM((planes, UP * lines, nx), F32),
+        in_specs=[smem, smem, smem, anywhere, anywhere],
+        out_specs=vmem,
         scratch_shapes=[
+            pltpu.VMEM((ny, nz, nx), F32),
+            pltpu.VMEM((ny, nz, nx), F32),
+            pltpu.VMEM((UP * lines, lines), BF),
             pltpu.VMEM((2, ny, nz + 2 * PAD, nx), BF),
             pltpu.VMEM((2, 2, ny // group, nz + 2 * PAD, nx), BF),
             pltpu.VMEM((2, 2, ny // group, nz, nx), BF),
@@ -298,21 +340,12 @@
             pltpu.VMEM((2, ny * 8, ny * 8), BF),
             pltpu.SemaphoreType.DMA((2, 8)),
             pltpu.SemaphoreType.DMA((2, 8)),
-            pltpu.SemaphoreType.DMA((ngz,)),
-            pltpu.SemaphoreType.DMA((ngz,)),
+            pltpu.SemaphoreType.DMA((ngz, 3)),
+            pltpu.SemaphoreType.DMA((ngz, 3)),
+            pltpu.SemaphoreType.DMA((2,)),
         ],
         compiler_params=pltpu.CompilerParams(collective_id=0, has_side_effects=True),
-    )(view_index, psf_taps, extents, estimate, measured)
-    return pl.pallas_call(
-        upsample_kernel,
-        grid=(planes,),
-        out_shape=jax.ShapeDtypeStruct((planes, UP * lines, nx), F32),
-        in_specs=[
-            pl.BlockSpec((UP * lines, lines), lambda y: (0, 0)),
-            pl.BlockSpec((1, lines, nx), lambda y: (y, 0, 0)),
-        ],
-        out_specs=pl.BlockSpec((1, UP * lines, nx), lambda y: (y, 0, 0)),
-    )(table, gathered)
+    )(view_index, psf_taps, extents.T, estimate, measured)
 
 
 def solution(mesh):

time: 32 us -> 28 us (0.88)
  Pallas kernels: 29.6 us -> 25.8 us
    pallas_call x2 -> x1, Pallas kernels: 29.6 us -> 25.8 us  [on_device(): pl.pallas_call(functools.partial(kernel, ngx, ngz), out_shape=pltpu.VMEM(...]
where the time goes in v2:
time: 28 us; the launch traced here: 27.7 us
  Pallas kernels  25.8 us (92%)
  local copies, waits for them, and re-layouts  1.32 us (5%)
  between operations  0.66 us (2%)
    pallas_call x1, Pallas kernels, on_device(): pl.pallas_call(functools.partial(kernel, ngx, ngz), out_shape=pltpu.VMEM(...  25.8 us
    unnamed x1, local copies, waits for them, and re-layouts  1.32 us

profile of v2, /device:TPU:0, one launch (start us, length us, event | category | flops | bytes accessed | tf_op | source)
XLA Modules:
  0.0 27.7 jit_solution(8100976872559775041)
XLA Ops:
  0.7 25.8 %shard_map.55 = f32[4,1024,128]{2,1,0:T(8,128)S(1)} custom-call(s32[1]{0:T(128)S(6)} %copy.8.view_ref, f32[6,3,31]{2,1,0:T(4,128)} %taps_ref.1, s32[3,6]{1,0:T(4,128)} %bitcast.1, f32[16,64,128]{2,1,0:T(8,128)} %est_hbm.1, f32[16,64,128]{2,1,0:T(8,128)} %mea_hbm.1), custom_call_target="tpu_custom_call" | custom-call | tf_op jit(solution)/shard_map/pallas_call | solution.py:321
  26.4 1.3 %copy.7 = f32[4,1024,128]{2,1,0:T(8,128)} copy(f32[4,1024,128]{2,1,0:T(8,128)S(1)} %shard_map.55) | data formatting | bytes 4194304

commit v3 on v2

--- a/solution.py
+++ b/solution.py
@@ -96,23 +96,34 @@
         packed[1, g] = right.astype(BF)
 
 
-def blur_rows(start, count, ext, side, mz, too, wide, ky, held, ny, nx):
+def blur_rows(blocks, near, m, ext, side, too, wide, ky, ny, nx):
     group = nx // PAD
-    reach = count + 2 * PAD
-    m = mz[0:count, 0:reach]
-    near = pl.ds(start, reach)
-    s = [
-        jnp.concatenate([dot(m, side[q, g, near, :]) for q in range(2)], axis=1).astype(BF)
-        for g in range(ny // group)
+    lots = ny // group
+    count = m.shape[0]
+    lines = [ext[y, near, :] for y in range(ny)]
+    lines += [side[q, g, near, :] for g in range(lots) for q in range(2)]
+    along_z = dot(m, jnp.concatenate(lines, axis=1))
+    own = jnp.concatenate([along_z[:, y * nx : (y + 1) * nx] for y in range(ny)], axis=0)
+    rim = jnp.concatenate(
+        [along_z[:, (ny + 2 * g) * nx : (ny + 2 * g + 2) * nx] for g in range(lots)], axis=0
+    )
+    rim = dot(rim.astype(BF), wide[...])
+    rim = jnp.concatenate(
+        [
+            rim[g * count : (g + 1) * count, j * nx : (j + 1) * nx]
+            for g in range(lots)
+            for j in range(group)
+        ],
+        axis=0,
+    )
+    along_x = (dot(own.astype(BF), too[...]) + rim).reshape(ny, count, nx)
+    slabs = [
+        along_x[:, k * 8 : (k + 1) * 8, :].reshape(ny * 8, nx) for k in range(count // 8)
     ]
-    vs = [dot(part, wide[...]) for part in s]
-    for y in range(ny):
-        u = dot(m, ext[y, near, :]).astype(BF)
-        g, j = divmod(y, group)
-        held[y, pl.ds(start, count), :] = dot(u, too[...]) + vs[g][:, j * nx : (j + 1) * nx]
-    for k in range(start // 8, (start + count) // 8):
-        a = held[:, k * 8 : (k + 1) * 8, :].reshape(ny * 8, nx).astype(BF)
-        yield pl.ds(k * 8, 8), dot(ky[...], a).reshape(ny, 8, nx)
+    result = dot(ky[...], jnp.concatenate(slabs, axis=1).astype(BF))
+    starts = [first + i for first, size in blocks for i in range(0, size, 8)]
+    for k, start in enumerate(starts):
+        yield pl.ds(start, 8), result[:, k * nx : (k + 1) * nx].reshape(ny, 8, nx)
 
 
 def kernel(
@@ -239,11 +250,16 @@
         )
 
     def blurred(r, blocks):
-        for first, count in blocks:
-            yield from blur_rows(
-                first, count, ext.at[r], side.at[r],
-                mz.at[r], too.at[r], wide.at[r], ky.at[r], held, ny, nx,
-            )
+        if len(blocks) == 1:
+            first, count = blocks[0]
+            near = pl.ds(first, count + 2 * PAD)
+            m = mz[r, 0:count, 0 : count + 2 * PAD]
+        else:
+            near = pl.ds(0, nz + 2 * PAD)
+            m = jnp.concatenate([mz[r, first : first + count, :] for first, count in blocks], axis=0)
+        yield from blur_rows(
+            blocks, near, m, ext.at[r], side.at[r], too.at[r], wide.at[r], ky.at[r], ny, nx
+        )
 
     def quotients(blocks):
         for rows, value in blurred(0, blocks):

time: 28 us -> 23.4 us (0.84)
  Pallas kernels: 25.8 us -> 21.2 us
    pallas_call x1, Pallas kernels: 25.8 us -> 21.2 us  [on_device(): pl.pallas_call(functools.partial(kernel, ngx, ngz), out_shape=pltpu.VMEM(...]
where the time goes in v3:
time: 23.4 us; the launch traced here: 23.1 us
  Pallas kernels  21.2 us (91%)
  local copies, waits for them, and re-layouts  1.32 us (6%)
  between operations  0.66 us (3%)
    pallas_call x1, Pallas kernels, on_device(): pl.pallas_call(functools.partial(kernel, ngx, ngz), out_shape=pltpu.VMEM(...  21.2 us
    unnamed x1, local copies, waits for them, and re-layouts  1.32 us

profile of v3, /device:TPU:0, one launch (start us, length us, event | category | flops | bytes accessed | tf_op | source)
XLA Modules:
  0.0 23.1 jit_solution(6599760892822542648)
XLA Ops:
  0.7 21.2 %shard_map.55 = f32[4,1024,128]{2,1,0:T(8,128)S(1)} custom-call(s32[1]{0:T(128)S(6)} %copy.8.view_ref, f32[6,3,31]{2,1,0:T(4,128)} %taps_ref.1, s32[3,6]{1,0:T(4,128)} %bitcast.1, f32[16,64,128]{2,1,0:T(8,128)} %est_hbm.1, f32[16,64,128]{2,1,0:T(8,128)} %mea_hbm.1), custom_call_target="tpu_custom_call" | custom-call | tf_op jit(solution)/shard_map/pallas_call | solution.py:337
  21.8 1.3 %copy.7 = f32[4,1024,128]{2,1,0:T(8,128)} copy(f32[4,1024,128]{2,1,0:T(8,128)S(1)} %shard_map.55) | data formatting | bytes 4194304

commit v4 on v3

--- a/solution.py
+++ b/solution.py
@@ -48,9 +48,15 @@
 
 def make_matrices(taps_ref, view, extents_ref, flip, mz, too, wide, ky, ny, nz, nx):
     group = nx // PAD
-    mz[...] = slanted(tap_row(taps_ref, view, extents_ref, 2, nx, 1, flip), nz, 1)[
-        :, : nz + 2 * PAD
-    ].astype(BF)
+    if flip:
+        lines = mz.shape[0]
+        full = slanted(tap_row(taps_ref, view, extents_ref, 2, lines, 1, flip), lines, -HALF)
+        away = jnp.abs(lanes_of((lines, lines)) - rows_of((lines, lines)))
+        mz[...] = jnp.where(away <= HALF, full, 0.0).astype(BF)
+    else:
+        mz[...] = slanted(tap_row(taps_ref, view, extents_ref, 2, nx, 1, flip), nz, 1)[
+            :, : nz + 2 * PAD
+        ].astype(BF)
     ring = slanted(tap_row(taps_ref, view, extents_ref, 0, nx, 1, not flip), nx, -HALF)
     lane, row = lanes_of((nx, nx)), rows_of((nx, nx))
     too[...] = jnp.where(jnp.abs(lane - row) <= HALF, ring, 0.0).astype(BF)
@@ -96,6 +102,25 @@
         packed[1, g] = right.astype(BF)
 
 
+def passes_xy(own, rim, too, wide, ky, ny, count, nx):
+    group = nx // PAD
+    lots = ny // group
+    rim = dot(rim, wide[...])
+    rim = jnp.concatenate(
+        [
+            rim[g * count : (g + 1) * count, j * nx : (j + 1) * nx]
+            for g in range(lots)
+            for j in range(group)
+        ],
+        axis=0,
+    )
+    along_x = (dot(own, too[...]) + rim).reshape(ny, count, nx)
+    slabs = [
+        along_x[:, k * 8 : (k + 1) * 8, :].reshape(ny * 8, nx) for k in range(count // 8)
+    ]
+    return dot(ky[...], jnp.concatenate(slabs, axis=1).astype(BF))
+
+
 def blur_rows(blocks, near, m, ext, side, too, wide, ky, ny, nx):
     group = nx // PAD
     lots = ny // group
@@ -107,20 +132,7 @@
     rim = jnp.concatenate(
         [along_z[:, (ny + 2 * g) * nx : (ny + 2 * g + 2) * nx] for g in range(lots)], axis=0
     )
-    rim = dot(rim.astype(BF), wide[...])
-    rim = jnp.concatenate(
-        [
-            rim[g * count : (g + 1) * count, j * nx : (j + 1) * nx]
-            for g in range(lots)
-            for j in range(group)
-        ],
-        axis=0,
-    )
-    along_x = (dot(own.astype(BF), too[...]) + rim).reshape(ny, count, nx)
-    slabs = [
-        along_x[:, k * 8 : (k + 1) * 8, :].reshape(ny * 8, nx) for k in range(count // 8)
-    ]
-    result = dot(ky[...], jnp.concatenate(slabs, axis=1).astype(BF))
+    result = passes_xy(own.astype(BF), rim.astype(BF), too, wide, ky, ny, count, nx)
     starts = [first + i for first, size in blocks for i in range(0, size, 8)]
     for k, start in enumerate(starts):
         yield pl.ds(start, 8), result[:, k * nx : (k + 1) * nx].reshape(ny, 8, nx)
@@ -131,9 +143,9 @@
     view_ref, taps_ref, extents_ref, est_hbm, mea_hbm,
     out_ref,
     est_ref, mea_ref, table_ref,
-    ext, side, packed, gathered, leaving, held, quot,
-    mz, too, wide, ky,
-    send_sem, recv_sem, all_send, all_recv, load_sem,
+    ext, side, packed, quot, rim_out, rim_in, leaving, gathered, est_lines,
+    mz, mz_all, too, wide, ky,
+    send_sem, recv_sem, rim_send, rim_recv, all_send, all_recv, load_sem,
 ):
     load_est = pltpu.make_async_copy(est_hbm, est_ref, load_sem.at[0])
     load_mea = pltpu.make_async_copy(mea_hbm, mea_ref, load_sem.at[1])
@@ -174,20 +186,20 @@
         first, count = {-1: (0, PAD), 0: (PAD, nz), 1: (PAD + nz, PAD)}[dz]
         rows = pl.ds(first, count)
         if dx == 0:
-            return ext.at[r, :, rows, :]
-        return side.at[r, 0 if dx < 0 else 1, :, rows, :]
+            return ext.at[:, rows, :]
+        return side.at[0 if dx < 0 else 1, :, rows, :]
 
     def copy(r, dx, dz):
         first, count = {-1: (0, PAD), 0: (0, nz), 1: (nz - PAD, PAD)}[dz]
         if dx == 0:
-            src = ext.at[r, :, pl.ds(PAD + first, count), :]
+            src = ext.at[:, pl.ds(PAD + first, count), :]
         else:
-            src = packed.at[r, 0 if dx < 0 else 1, :, pl.ds(first, count), :]
+            src = packed.at[0 if dx < 0 else 1, :, pl.ds(first, count), :]
         return pltpu.make_async_remote_copy(
             src_ref=src,
             dst_ref=landing(r, -dx, -dz),
-            send_sem=send_sem.at[r, AROUND.index((dx, dz))],
-            recv_sem=recv_sem.at[r, AROUND.index((-dx, -dz))],
+            send_sem=send_sem.at[AROUND.index((dx, dz))],
+            recv_sem=recv_sem.at[AROUND.index((-dx, -dz))],
             device_id=(gx + dx, gz + dz),
             device_id_type=MESH,
         )
@@ -198,8 +210,8 @@
         return pltpu.make_async_remote_copy(
             src_ref=dst,
             dst_ref=dst,
-            send_sem=send_sem.at[r, AROUND.index((dx, dz))],
-            recv_sem=recv_sem.at[r, AROUND.index((dx, dz))],
+            send_sem=send_sem.at[AROUND.index((dx, dz))],
+            recv_sem=recv_sem.at[AROUND.index((dx, dz))],
             device_id=(gx + dx, gz + dz),
             device_id_type=MESH,
         )
@@ -232,105 +244,170 @@
     above = [(0, -1), (0, 1)]
     sideways = [(-1, 0), (1, 0)]
     corners = [d for d in AROUND if d[0] and d[1]]
-    middle = [(PAD, nz - 2 * PAD)]
-    ends = [(0, PAD), (nz - PAD, PAD)]
-    parts = middle + ends
-
-    def exchange(d, part):
+    parts = [[(PAD, nz - 2 * PAD)], [(0, PAD), (nz - PAD, PAD)]]
+    counts = [nz - 2 * PAD, 2 * PAD]
+    lots = packed.shape[1]
+
+    def rim_copy(p, dx):
+        rows = pl.ds(0, counts[p])
+        return pltpu.make_async_remote_copy(
+            src_ref=rim_out.at[p, 0 if dx < 0 else 1, :, rows, :],
+            dst_ref=rim_in.at[p, 1 if dx < 0 else 0, :, rows, :],
+            send_sem=rim_send.at[p, 0 if dx < 0 else 1],
+            recv_sem=rim_recv.at[p, 1 if dx < 0 else 0],
+            device_id=(gx + dx, gz),
+            device_id_type=MESH,
+        )
+
+    def rim_arrival(p, dx):
+        dst = rim_in.at[p, 0 if dx < 0 else 1, :, pl.ds(0, counts[p]), :]
+        return pltpu.make_async_remote_copy(
+            src_ref=dst,
+            dst_ref=dst,
+            send_sem=rim_send.at[p, 0 if dx < 0 else 1],
+            recv_sem=rim_recv.at[p, 0 if dx < 0 else 1],
+            device_id=(gx + dx, gz),
+            device_id_type=MESH,
+        )
+
+    def exchange(d, p):
         to = lax.rem(gz + d, ngz)
-        first, count = parts[part]
-        there_rows = pl.ds(pl.multiple_of(gz * nz + first, PAD), count)
+        theirs = pl.ds(to * planes, planes)
+        if p == 2:
+            src = est_out(theirs)
+            dst = est_lines.at[:, pl.ds(pl.multiple_of(gz * nz, nz), nz), :]
+        else:
+            src = leaving.at[p, theirs, pl.ds(0, counts[p]), :]
+            dst = gathered.at[p, gz, :, pl.ds(0, counts[p]), :]
         return pltpu.make_async_remote_copy(
-            src_ref=leaving.at[pl.ds(to * planes, planes), pl.ds(first, count), :],
-            dst_ref=gathered.at[:, there_rows, :],
-            send_sem=all_send.at[d, part],
-            recv_sem=all_recv.at[d, part],
+            src_ref=src,
+            dst_ref=dst,
+            send_sem=all_send.at[d, p],
+            recv_sem=all_recv.at[d, p],
             device_id=(gx, to),
             device_id_type=MESH,
         )
 
-    def blurred(r, blocks):
-        if len(blocks) == 1:
+    def est_out(which):
+        return ext.at[which, pl.ds(PAD, nz), :]
+
+    def quotients(p):
+        blocks = parts[p]
+        if p == 0:
             first, count = blocks[0]
             near = pl.ds(first, count + 2 * PAD)
-            m = mz[r, 0:count, 0 : count + 2 * PAD]
+            m = mz[0:count, 0 : count + 2 * PAD]
         else:
             near = pl.ds(0, nz + 2 * PAD)
-            m = jnp.concatenate([mz[r, first : first + count, :] for first, count in blocks], axis=0)
-        yield from blur_rows(
-            blocks, near, m, ext.at[r], side.at[r], too.at[r], wide.at[r], ky.at[r], ny, nx
-        )
-
-    def quotients(blocks):
-        for rows, value in blurred(0, blocks):
-            quot[:, rows, :] = mea_ref[:, rows, :] / value
-        for first, count in blocks:
-            ext[1, :, PAD + first : PAD + first + count, :] = quot[
-                :, first : first + count, :
-            ].astype(BF)
-
-    def products(blocks):
-        for rows, value in blurred(1, blocks):
-            held[:, rows, :] = est_ref[:, rows, :] * value
-        for first, count in blocks:
-            rows = slice(first, first + count)
-            leaving[:, rows, :] = held[:, rows, :].astype(BF)
+            m = jnp.concatenate([mz[first : first + count, :] for first, count in blocks], axis=0)
+        at = 0
+        for rows, value in blur_rows(
+            blocks, near, m, ext, side, too.at[0], wide.at[0], ky.at[0], ny, nx
+        ):
+            quot[p, :, at : at + 8, :] = mea_ref[:, rows, :] / value
+            at += 8
+        count = counts[p]
+        pack_edges(
+            lambda y: quot[p, y, :count, :], rim_out.at[p, :, :, pl.ds(0, count), :], ny, count, nx
+        )
+        for dx in (-1, 1):
+            @pl.when(has_x[dx])
+            def _(dx=dx):
+                rim_copy(p, dx).start()
+
+            @pl.when(jnp.logical_not(has_x[dx]))
+            def _(dx=dx):
+                spot = rim_in.at[p, 0 if dx < 0 else 1]
+                spot[...] = jnp.zeros(spot.shape, BF)
+
+    def regroup(p):
+        for dx in (-1, 1):
+            @pl.when(has_x[dx])
+            def _(dx=dx):
+                rim_arrival(p, dx).wait_recv()
+        count = counts[p]
+        own = quot[p, :, :count, :].reshape(ny * count, nx).astype(BF)
+        rim = jnp.concatenate(
+            [
+                jnp.concatenate([rim_in[p, q, g, :count, :] for q in range(2)], axis=1)
+                for g in range(lots)
+            ],
+            axis=0,
+        )
+        result = passes_xy(own, rim, too.at[1], wide.at[1], ky.at[1], ny, count, nx)
+        for k in range(count // PAD):
+            pair = [
+                result[:, i * nx : (i + 1) * nx].reshape(ny, 8, nx) for i in (2 * k, 2 * k + 1)
+            ]
+            leaving[p, :, k * PAD : (k + 1) * PAD, :] = jnp.concatenate(pair, axis=1).astype(BF)
+        for d in range(1, ngz):
+            exchange(d, p).start()
+        gathered[p, gz, :, :count, :] = leaving[p, pl.ds(gz * planes, planes), :count, :]
 
     load_est.wait()
-    ext[0, :, PAD : PAD + nz, :] = est_ref[...].astype(BF)
+    ext[:, PAD : PAD + nz, :] = est_ref[...].astype(BF)
     pl.semaphore_wait(barrier, total)
     send(0, above)
-    pack_edges(lambda y: est_ref[y], packed.at[0], ny, nz, nx)
+    pack_edges(lambda y: est_ref[y], packed, ny, nz, nx)
     send(0, corners + sideways)
+    for d in range(1, ngz):
+        exchange(d, 2).start()
     view = view_ref[0]
     for flip in range(2):
         make_matrices(
             taps_ref, view, extents_ref, bool(flip),
-            mz.at[flip], too.at[flip], wide.at[flip], ky.at[flip], ny, nz, nx,
+            mz_all if flip else mz, too.at[flip], wide.at[flip], ky.at[flip], ny, nz, nx,
         )
     clear(0)
-    clear(1)
     load_mea.wait()
     receive(0, sideways)
-    quotients(middle)
+    quotients(0)
+    make_table(table_ref, nz * ngz)
+    est_lines[:, pl.ds(pl.multiple_of(gz * nz, nz), nz), :] = ext[
+        pl.ds(gz * planes, planes), PAD : PAD + nz, :
+    ]
+    regroup(0)
     receive(0, above + corners)
-    quotients(ends)
-    send(1, above)
-    pack_edges(lambda y: quot[y], packed.at[1], ny, nz, nx)
-    send(1, corners + sideways)
-    make_table(table_ref, nz * ngz)
-    receive(1, sideways)
-    products(middle)
+    quotients(1)
+    regroup(1)
     for d in range(1, ngz):
-        exchange(d, 0).start()
-    receive(1, above + corners)
-    products(ends)
-    for d in range(1, ngz):
-        for part in (1, 2):
-            exchange(d, part).start()
-    mine = pl.ds(pl.multiple_of(gz * nz, nz), nz)
-    gathered[:, mine, :] = leaving[pl.ds(gz * planes, planes)]
-    for d in range(1, ngz):
-        for part in range(3):
-            exchange(d, part).wait_recv()
-    lines = jnp.concatenate([gathered[y] for y in range(planes)], axis=1)
+        for p in (2, 0, 1):
+            exchange(d, p).wait_recv()
+    lines = []
+    for y in range(planes):
+        line = []
+        for g in range(ngz):
+            line += [
+                gathered[1, g, y, :PAD, :],
+                gathered[0, g, y, : counts[0], :],
+                gathered[1, g, y, PAD : 2 * PAD, :],
+            ]
+        lines.append(jnp.concatenate(line, axis=0))
+    correction = dot(mz_all[...], jnp.concatenate(lines, axis=1))
+    estimate = jnp.concatenate([est_lines[y] for y in range(planes)], axis=1)
+    rounded = (estimate.astype(F32) * correction).astype(BF)
     step = nz * ngz
     for b in range(UP):
         rows = slice(b * step, (b + 1) * step)
-        whole = dot(table_ref[rows, :], lines)
+        whole = dot(table_ref[rows, :], rounded)
         for y in range(planes):
             out_ref[y, rows, :] = whole[:, y * nx : (y + 1) * nx]
     sent(0)
-    sent(1)
+    for p in range(2):
+        for dx in (-1, 1):
+            @pl.when(has_x[dx])
+            def _(p=p, dx=dx):
+                rim_copy(p, dx).wait_send()
     for d in range(1, ngz):
-        for part in range(3):
-            exchange(d, part).wait_send()
+        for p in range(3):
+            exchange(d, p).wait_send()
 
 
 def on_device(ngx, ngz, view_index, psf_taps, extents, estimate, measured):
     ny, nz, nx = estimate.shape
     planes, lines = ny // ngz, nz * ngz
     group = nx // PAD
+    half = max(2 * PAD, nz - 2 * PAD)
     smem = pl.BlockSpec(memory_space=pltpu.SMEM)
     vmem = pl.BlockSpec(memory_space=pltpu.VMEM)
     anywhere = pl.BlockSpec(memory_space=pl.ANY)
@@ -343,19 +420,24 @@
             pltpu.VMEM((ny, nz, nx), F32),
             pltpu.VMEM((ny, nz, nx), F32),
             pltpu.VMEM((UP * lines, lines), BF),
-            pltpu.VMEM((2, ny, nz + 2 * PAD, nx), BF),
-            pltpu.VMEM((2, 2, ny // group, nz + 2 * PAD, nx), BF),
-            pltpu.VMEM((2, 2, ny // group, nz, nx), BF),
+            pltpu.VMEM((ny, nz + 2 * PAD, nx), BF),
+            pltpu.VMEM((2, ny // group, nz + 2 * PAD, nx), BF),
+            pltpu.VMEM((2, ny // group, nz, nx), BF),
+            pltpu.VMEM((2, ny, half, nx), F32),
+            pltpu.VMEM((2, 2, ny // group, half, nx), BF),
+            pltpu.VMEM((2, 2, ny // group, half, nx), BF),
+            pltpu.VMEM((2, ny, half, nx), BF),
+            pltpu.VMEM((2, ngz, planes, half, nx), BF),
             pltpu.VMEM((planes, lines, nx), BF),
-            pltpu.VMEM((ny, nz, nx), BF),
-            pltpu.VMEM((ny, nz, nx), F32),
-            pltpu.VMEM((ny, nz, nx), F32),
-            pltpu.VMEM((2, nz, nz + 2 * PAD), BF),
+            pltpu.VMEM((nz, nz + 2 * PAD), BF),
+            pltpu.VMEM((lines, lines), BF),
             pltpu.VMEM((2, nx, nx), BF),
             pltpu.VMEM((2, 2 * nx, group * nx), BF),
             pltpu.VMEM((2, ny * 8, ny * 8), BF),
-            pltpu.SemaphoreType.DMA((2, 8)),
-            pltpu.SemaphoreType.DMA((2, 8)),
+            pltpu.SemaphoreType.DMA((8,)),
+            pltpu.SemaphoreType.DMA((8,)),
+            pltpu.SemaphoreType.DMA((2, 2)),
+            pltpu.SemaphoreType.DMA((2, 2)),
             pltpu.SemaphoreType.DMA((ngz, 3)),
             pltpu.SemaphoreType.DMA((ngz, 3)),
             pltpu.SemaphoreType.DMA((2,)),

time: 23.4 us -> 20.9 us (0.89)
  the two profiles are of different devices: /device:TPU:0 before, /device:TPU:9 now
where the time goes in v4:
time: 20.9 us; the launch traced here: 20.7 us
  Pallas kernels  18.7 us (89%)
  local copies, waits for them, and re-layouts  1.32 us (6%)
  between operations  0.66 us (3%)
    pallas_call x1, Pallas kernels, on_device(): pl.pallas_call(functools.partial(kernel, ngx, ngz), out_shape=pltpu.VMEM(...  18.7 us
    unnamed x1, local copies, waits for them, and re-layouts  1.32 us

profile of v4, /device:TPU:9, one launch (start us, length us, event | category | flops | bytes accessed | tf_op | source)
XLA Modules:
  0.0 20.7 jit_solution(6301138762176801149)
XLA Ops:
  0.7 18.7 %shard_map.55 = f32[4,1024,128]{2,1,0:T(8,128)S(1)} custom-call(s32[1]{0:T(128)S(6)} %copy.8.view_ref, f32[6,3,31]{2,1,0:T(4,128)} %taps_ref.1, s32[3,6]{1,0:T(4,128)} %bitcast.1, f32[16,64,128]{2,1,0:T(8,128)} %est_hbm.1, f32[16,64,128]{2,1,0:T(8,128)} %mea_hbm.1), custom_call_target="tpu_custom_call" | custom-call | tf_op jit(solution)/shard_map/pallas_call | solution.py:414
  19.3 1.3 %copy.7 = f32[4,1024,128]{2,1,0:T(8,128)} copy(f32[4,1024,128]{2,1,0:T(8,128)S(1)} %shard_map.55) | data formatting | bytes 4194304

commit v5 on v4

--- a/solution.py
+++ b/solution.py
@@ -350,8 +350,6 @@
     send(0, above)
     pack_edges(lambda y: est_ref[y], packed, ny, nz, nx)
     send(0, corners + sideways)
-    for d in range(1, ngz):
-        exchange(d, 2).start()
     view = view_ref[0]
     for flip in range(2):
         make_matrices(
@@ -362,6 +360,8 @@
     load_mea.wait()
     receive(0, sideways)
     quotients(0)
+    for d in range(1, ngz):
+        exchange(d, 2).start()
     make_table(table_ref, nz * ngz)
     est_lines[:, pl.ds(pl.multiple_of(gz * nz, nz), nz), :] = ext[
         pl.ds(gz * planes, planes), PAD : PAD + nz, :

time: 20.9 us -> 20.9 us (level)
  the two profiles are of different devices: /device:TPU:9 before, /device:TPU:17 now
where the time goes in v5:
time: 20.9 us; the launch traced here: 20.7 us
  Pallas kernels  18.7 us (89%)
  local copies, waits for them, and re-layouts  1.32 us (6%)
  between operations  0.66 us (3%)
    pallas_call x1, Pallas kernels, on_device(): pl.pallas_call(functools.partial(kernel, ngx, ngz), out_shape=pltpu.VMEM(...  18.7 us
    unnamed x1, local copies, waits for them, and re-layouts  1.32 us

profile of v5, /device:TPU:17, one launch (start us, length us, event | category | flops | bytes accessed | tf_op | source)
XLA Modules:
  0.0 20.7 jit_solution(13673180710960218659)
XLA Ops:
  0.7 18.7 %shard_map.55 = f32[4,1024,128]{2,1,0:T(8,128)S(1)} custom-call(s32[1]{0:T(128)S(6)} %copy.8.view_ref, f32[6,3,31]{2,1,0:T(4,128)} %taps_ref.1, s32[3,6]{1,0:T(4,128)} %bitcast.1, f32[16,64,128]{2,1,0:T(8,128)} %est_hbm.1, f32[16,64,128]{2,1,0:T(8,128)} %mea_hbm.1), custom_call_target="tpu_custom_call" | custom-call | tf_op jit(solution)/shard_map/pallas_call | solution.py:414
  19.3 1.3 %copy.7 = f32[4,1024,128]{2,1,0:T(8,128)} copy(f32[4,1024,128]{2,1,0:T(8,128)S(1)} %shard_map.55) | data formatting | bytes 4194304
